TPU v7x, 32 devices: a whole 2x2x4 slice. The times are simulated.
32 devices in a mesh: section: 4 (over z), fsdp: 4 (over y, core), tp: 2 (over x).
Axes of the slice: x: 2, y: 2, z: 4, core: 2. Of those that a mesh axis runs over, the one named last changes fastest.
Arguments:
- stash: bfloat16 [4, 4, 512, 2304], P('section', None, 'fsdp'), may hold values from -6 to 6
- grad_now: bfloat16 [4, 512, 2304], P('section', 'fsdp'), may hold values from -6 to 6
- grad_top: bfloat16 [2, 512, 2304], P(None, 'fsdp'), may hold values from -6 to 6
- order: int32 [4, 4], P('section'), may hold values from 0 to 3, each once within a row
- gain: float32 [4, 2304], P('section'), may hold values from 0.5 to 1.5
- weight: bfloat16 [4, 2304, 2048], P('section', 'fsdp', 'tp'), may hold values from -0.125 to 0.125
Outputs:
- grad_held: bfloat16 [4, 512, 2304], P('section', 'fsdp')
- weight_grad: float32 [4, 2304, 2048], P('section', 'fsdp', 'tp')
Inputs may be any that keep to these rules, and one draw needn't show every extreme that they name: Each row of order names every kept micro-batch once.
All inputs are finite; a program needn't handle non-finite values.
Results may differ from a plain program's by a relative error of at most 0.013.
Values may be sent and summed in bfloat16 or wider, within the bound.
A program may use at most 64 MiB of HBM per device.

v0:
```python
import jax
import jax.numpy as jnp
from jax import lax
from jax.sharding import PartitionSpec as P

norm_eps = 1e-06


def shifted(shard, axis, by):
    length = lax.axis_size(axis)
    pairs = [(i, i + by) for i in range(length) if 0 <= i + by < length]
    return lax.ppermute(shard, axis, pairs)


def gelu_tanh(values):
    return jax.nn.gelu(values, approximate=True)


def per_device(stash, grad_now, grad_top, order, gain, weight):
    full_weight = lax.all_gather(weight[0], "fsdp", axis=0, tiled=True)
    section_gain = gain[0]
    is_last = lax.axis_index("section") == lax.axis_size("section") - 1
    tp_count = lax.axis_size("tp")
    tp_place = lax.axis_index("tp")
    feature_count = stash.shape[-1]
    share_width = feature_count // tp_count
    share_start = tp_place * share_width
    rows_here = grad_now.shape[1]
    grad_in = grad_now[0]
    lhs_parts = []
    rhs_parts = []
    for tick_id in range(grad_top.shape[0]):
        slot_id = order[0, tick_id]
        section_in = lax.dynamic_index_in_dim(stash[0], slot_id, 0, keepdims=False)
        values = section_in.astype(jnp.float32)
        inv_rms = lax.rsqrt(jnp.mean(values * values, axis=-1, keepdims=True) + norm_eps)
        scaled = values * inv_rms
        normed = (scaled * section_gain).astype(jnp.bfloat16)
        stacked = jnp.concatenate([normed, grad_in], axis=0)
        products = jnp.dot(stacked, full_weight, preferred_element_type=jnp.float32)
        hidden = products[:rows_here]
        backed = products[rows_here:]
        activated, pullback = jax.vjp(gelu_tanh, hidden)
        grad_pre = pullback(backed)[0].astype(jnp.bfloat16)
        activated = activated.astype(jnp.bfloat16)
        lhs_parts.append(normed)
        lhs_parts.append(grad_in)
        rhs_parts.append(grad_pre)
        rhs_parts.append(activated)
        partial_dh = lax.dot_general(
            grad_pre, full_weight, (((1,), (1,)), ((), ())), preferred_element_type=jnp.float32
        )
        total_share = lax.psum_scatter(
            partial_dh.astype(jnp.bfloat16), "tp", scatter_dimension=1, tiled=True
        ).astype(jnp.float32)
        scaled_share = lax.dynamic_slice_in_dim(scaled, share_start, share_width, 1)
        gain_share = lax.dynamic_slice_in_dim(section_gain, share_start, share_width, 0)
        grad_share = lax.dynamic_slice_in_dim(grad_in, share_start, share_width, 1)
        gained = gain_share * total_share
        moment_sum = lax.psum(jnp.sum(gained * scaled_share, axis=-1), "tp")
        inner_mean = (moment_sum / feature_count)[:, None]
        out_share = (
            grad_share.astype(jnp.float32) + inv_rms * (gained - scaled_share * inner_mean)
        ).astype(jnp.bfloat16)
        arrived = shifted(out_share, "section", -1)
        top_share = lax.dynamic_slice_in_dim(grad_top[tick_id], share_start, share_width, 1)
        held_share = jnp.where(is_last, top_share, arrived)
        grad_in = lax.all_gather(held_share, "tp", axis=1, tiled=True)
    lhs_all = jnp.concatenate(lhs_parts, axis=0)
    rhs_all = jnp.concatenate(rhs_parts, axis=0)
    weight_grad = lax.psum_scatter(
        lax.dot_general(
            lhs_all, rhs_all, (((0,), (0,)), ((), ())), preferred_element_type=jnp.float32
        ).astype(jnp.bfloat16),
        "fsdp",
        scatter_dimension=0,
        tiled=True,
    ).astype(jnp.float32)
    return (grad_in[None], weight_grad[None])


def solution(mesh):
    return jax.shard_map(
        per_device,
        mesh=mesh,
        in_specs=(
            P("section", None, "fsdp", None),
            P("section", "fsdp", None),
            P(None, "fsdp", None),
            P("section", None),
            P("section", None),
            P("section", "fsdp", "tp"),
        ),
        out_specs=(P("section", "fsdp", None), P("section", "fsdp", "tp")),
        check_vma=False,
    )
```

profile of v0, /device:TPU:0, one launch (start us, length us, event | category | flops | bytes accessed | tf_op | source)
XLA Modules:
  0.0 181.7 jit_solution(16638024135752744247)
XLA Ops:
  7.2 0.0 all-gather.3.cloned.1.call-start
  7.2 0.7 all-gather.3.cloned.1.call-update
  7.9 0.0 reduce-scatter.10.cloned.1.call-start
  7.9 1.3 fusion.55
  11.8 0.7 reduce.1
  13.9 1.6 fusion.22
  15.5 2.3 %multiply_convert_fusion = (bf16[128,2304]{1,0:T(8,128)(2,1)}, bf16[128,2304]{1,0:T(8,128)(2,1)S(1)}, f32[128,2304]{1,0:T(8,128)S(1)}, f32[128,2304]{1,0:T(8,128)S(1)}) fusion(f32[2304]{0:T(1024)S(1)} %reduce.1, f32[128]{0:T(128)S(1)} %get-tuple-element.16, bf16[1,4,128,2304]{3,2,1,0:T(8,128)(2,1)} %param.6, s32[]{:T(128)S(6)} %select_n.33, ...), kind=kLoop, calls=%fused_computation.31 | loop fusion | flops 2359296 | bytes 4728840 | tf_op jit(solution)/shard_map/convert_element_type | solution.py:38
  17.7 32.0 %all-gather.3.cloned.1.call-done = bf16[1,2304,1024]{2,1,0:T(8,128)(2,1)} async-done(((bf16[1,576,1024]{2,1,0:T(8,128)(2,1)}), bf16[1,2304,1024]{2,1,0:T(8,128)(2,1)}) %all-gather.3.cloned.1.call-update) | async-done | bytes 4718608 | tf_op jit(solution)/shard_map/all_gather | solution.py:20
  49.7 4.0 %fusion.6 = f32[256,1024]{1,0:T(8,128)S(1)} fusion(bf16[1,2304,1024]{2,1,0:T(8,128)(2,1)} %all-gather.3.cloned.1.call-done, bf16[128,2304]{1,0:T(8,128)(2,1)} %bitcast.52, bf16[128,2304]{1,0:T(8,128)(2,1)S(1)} %get-tuple-element.5), kind=kOutput, calls=%fused_computation.7 | convolution fusion | flops 1210318848 | bytes 6946816 | tf_op jit(solution)/shard_map/dot_general | solution.py:40
  53.8 1.1 multiply_convert_fusion.3
  54.9 1.7 fusion.8
  56.5 1.1 copy.8
  57.6 0.0 reduce-scatter.10.cloned.1.call-update
  57.6 0.0 reduce-scatter.12.cloned.1.call-start
  57.7 15.4 %reduce-scatter.10.cloned.1.call-done = bf16[1152,128]{1,0:T(8,128)(2,1)} async-done(((bf16[2304,128]{1,0:T(8,128)(2,1)}), bf16[1152,128]{1,0:T(8,128)(2,1)}) %reduce-scatter.10.cloned.1.call-update) | async-done | bytes 294928
  73.1 1.2 copy.9
  74.3 0.2 multiply_reduce_fusion.1
  74.5 4.9 %psum.14 = f32[128]{0:T(128)S(1)} all-reduce(f32[128]{0:T(128)S(1)} %multiply_reduce_fusion.1), channel_id=1, replica_groups=mesh['section'=4,'fsdp'=4,'tp'=2] {'tp'}, use_global_device_ids=true, to_apply=%region_3.4 | all-reduce | flops 128 | bytes 1024 | tf_op jit(solution)/shard_map/psum | solution.py:60
  79.4 1.3 fusion.36
  80.7 0.0 copy-start.2
  80.7 1.4 collective-permute-start
  82.1 0.0 copy-done.1
  82.1 0.1 fusion.54
  82.2 8.0 %collective-permute-done = bf16[128,1152]{1,0:T(8,128)(2,1)} collective-permute-done((bf16[128,1152]{1,0:T(8,128)(2,1)S(1)}, bf16[128,1152]{1,0:T(8,128)(2,1)}, u32[]{:S(2)}, u32[]{:S(2)}) %collective-permute-start) | collective-permute-done | bytes 294944 | tf_op jit(solution)/shard_map/ppermute | solution.py:12
  90.2 1.0 bitcast_select_fusion
  91.2 0.0 slice-start
  91.3 7.5 %all_gather.10 = bf16[128,2304]{1,0:T(8,128)(2,1)S(1)} all-gather(bf16[128,1152]{1,0:T(8,128)(2,1)S(1)} %bitcast_select_fusion), channel_id=1, replica_groups=mesh['section'=4,'fsdp'=4,'tp'=2] {'tp'}, dimensions={1}, use_global_device_ids=true | all-gather | bytes 884736 | tf_op jit(solution)/shard_map/all_gather | solution.py:68
  98.8 3.8 %fusion.2 = f32[256,1024]{1,0:T(8,128)S(1)} fusion(bf16[1,2304,1024]{2,1,0:T(8,128)(2,1)} %all-gather.3.cloned.1.call-done, bf16[128,2304]{1,0:T(8,128)(2,1)S(1)} %all_gather.10, bf16[128,2304]{1,0:T(8,128)(2,1)S(1)} %copy-done.2), kind=kOutput, calls=%fused_computation.3 | convolution fusion | flops 1210318848 | bytes 6946816 | tf_op jit(solution)/shard_map/dot_general | solution.py:40
  102.6 1.1 multiply_convert_fusion.2
  103.6 0.0 slice-done.1
  103.7 1.7 fusion.11
  105.3 1.1 copy.10
  106.4 0.0 reduce-scatter.12.cloned.1.call-update
  106.4 0.0 reduce-scatter.8.cloned.1.call-start
  106.5 6.3 %convolution_convert_fusion = bf16[2304,1024]{1,0:T(8,128)(2,1)} fusion(bf16[128,2304]{1,0:T(8,128)(2,1)S(1)} %all_gather.10, bf16[128,2304]{1,0:T(8,128)(2,1)} %get-tuple-element.4, bf16[128,2304]{1,0:T(8,128)(2,1)} %bitcast.53, bf16[128,2304]{1,0:T(8,128)(2,1)} %copy-done.3, bf16[128,1024]{1,0:T(8,128)(2,1)} %get-tuple-element.12, ...), kind=kOutput, calls=%fused_computation | convolution fusion | flops 2431909888 | bytes 8126464 | tf_op jit(solution)/shard_map/dot_general | solution.py:72
  112.8 0.0 reduce-scatter.8.cloned.1.call-update
  112.8 8.2 %reduce-scatter.12.cloned.1.call-done = bf16[1152,128]{1,0:T(8,128)(2,1)} async-done(((bf16[2304,128]{1,0:T(8,128)(2,1)}), bf16[1152,128]{1,0:T(8,128)(2,1)}) %reduce-scatter.12.cloned.1.call-update) | async-done | bytes 294928
  121.0 1.2 copy.11
  122.2 0.2 multiply_reduce_fusion
  122.3 4.9 %psum.15 = f32[128]{0:T(128)S(1)} all-reduce(f32[128]{0:T(128)S(1)} %multiply_reduce_fusion), channel_id=1, replica_groups=mesh['section'=4,'fsdp'=4,'tp'=2] {'tp'}, use_global_device_ids=true, to_apply=%region_7.8 | all-reduce | flops 128 | bytes 1024 | tf_op jit(solution)/shard_map/psum | solution.py:60
  127.3 0.2 add_convert_fusion
  127.5 1.3 collective-permute-start.1
  128.8 8.0 %collective-permute-done.1 = bf16[128,1152]{1,0:T(8,128)(2,1)S(1)} collective-permute-done((bf16[128,1152]{1,0:T(8,128)(2,1)S(1)}, bf16[128,1152]{1,0:T(8,128)(2,1)S(1)}, u32[]{:S(2)}, u32[]{:S(2)}) %collective-permute-start.1) | collective-permute-done | bytes 294944 | tf_op jit(solution)/shard_map/ppermute | solution.py:12
  136.8 0.1 bitcast_select_fusion.1
  136.9 7.4 %all_gather.11 = bf16[128,2304]{1,0:T(8,128)(2,1)S(1)} all-gather(bf16[128,1152]{1,0:T(8,128)(2,1)S(1)} %bitcast_select_fusion.1), channel_id=1, replica_groups=mesh['section'=4,'fsdp'=4,'tp'=2] {'tp'}, dimensions={1}, use_global_device_ids=true | all-gather | bytes 884736 | tf_op jit(solution)/shard_map/all_gather | solution.py:68
  144.3 27.2 %reduce-scatter.8.cloned.1.call-done = bf16[576,1024]{1,0:T(8,128)(2,1)} async-done(((bf16[2304,1024]{1,0:T(8,128)(2,1)}), bf16[576,1024]{1,0:T(8,128)(2,1)}) %reduce-scatter.8.cloned.1.call-update) | async-done | bytes 1179664 | tf_op jit(solution)/shard_map/reduce_scatter | solution.py:71
  171.4 3.0 %bitcast_convert_fusion = f32[1,576,1024]{2,1,0:T(8,128)} fusion(bf16[576,1024]{1,0:T(8,128)(2,1)} %reduce-scatter.8.cloned.1.call-done), kind=kLoop, calls=%fused_computation.30 | loop fusion | flops 589824 | bytes 3538944 | tf_op jit(solution)/shard_map/broadcast_in_dim | solution.py:79
  174.4 0.8 copy.13
  (15 shorter events, 0.1 us)
Async XLA Ops:
  7.2 42.6 %all-gather.3.cloned.1.call-start = ((), (), s32[]{:S(2)}) async-start(), calls=%async_computation.4 | async-start | bytes 5898240 | tf_op jit(solution)/shard_map/all_gather | solution.py:20
  7.9 65.2 %reduce-scatter.10.cloned.1.call-start = ((), (), s32[]{:S(2)}) async-start(), calls=%async_computation.5 | async-start | bytes 884736
  17.7 36.1 %copy-start.3 = (bf16[128,2304]{1,0:T(8,128)(2,1)}, bf16[128,2304]{1,0:T(8,128)(2,1)S(1)}, u32[]{:S(2)}) copy-start(bf16[128,2304]{1,0:T(8,128)(2,1)S(1)} %get-tuple-element.5) | copy-start | bytes 1769476
  49.7 5.1 %copy-start = (bf16[1,2304,1024]{2,1,0:T(8,128)(2,1)S(1)}, bf16[1,2304,1024]{2,1,0:T(8,128)(2,1)}, u32[]{:S(2)}) copy-start(bf16[1,2304,1024]{2,1,0:T(8,128)(2,1)} %all-gather.3.cloned.1.call-done) | copy-start | bytes 14155780
  54.9 2.8 %copy-start.4 = (f32[1,2304]{1,0:T(1,128)S(1)}, f32[1,2304]{1,0:T(1,128)}, u32[]{:S(2)}) copy-start(f32[1,2304]{1,0:T(1,128)} %param.10) | copy-start | bytes 27652
  57.6 63.4 %reduce-scatter.12.cloned.1.call-start = ((), (), s32[]{:S(2)}) async-start(), calls=%async_computation.6 | async-start | bytes 884736
  79.4 2.7 %copy-start.1 = (bf16[2,128,2304]{2,1,0:T(8,128)(2,1)S(1)}, bf16[2,128,2304]{2,1,0:T(8,128)(2,1)}, u32[]{:S(2)}) copy-start(bf16[2,128,2304]{2,1,0:T(8,128)(2,1)} %param.8) | copy-start | bytes 3538948
  80.7 18.1 %copy-start.2 = (bf16[128,2304]{1,0:T(8,128)(2,1)S(1)}, bf16[128,2304]{1,0:T(8,128)(2,1)}, u32[]{:S(2)}) copy-start(bf16[128,2304]{1,0:T(8,128)(2,1)} %get-tuple-element.4) | copy-start | bytes 1769476
  80.7 9.5 %collective-permute-start = (bf16[128,1152]{1,0:T(8,128)(2,1)S(1)}, bf16[128,1152]{1,0:T(8,128)(2,1)}, u32[]{:S(2)}, u32[]{:S(2)}) collective-permute-start(bf16[128,1152]{1,0:T(8,128)(2,1)S(1)} %fusion.36), channel_id=1, source_target_pairs={{8,0},{16,8},{24,16},{9,1},{17,9},{25,17},{10,2},{18,10},{26,18},{... | collective-permute-start | bytes 884744 | tf_op jit(solution)/shard_map/ppermute | solution.py:12
  91.2 12.4 %slice-start = ((s8[4718592]{0:T(1024)(128)(4,1)}), s8[4194304]{0:T(1024)(128)(4,1)S(1)}, s32[]{:S(2)}) async-start(s8[4718592]{0:T(1024)(128)(4,1)} %bitcast.45), calls=%async_computation.7 | async-start | bytes 8388608
  98.8 4.9 %slice-start.1 = ((s8[4718592]{0:T(1024)(128)(4,1)}), s8[524288]{0:T(1024)(128)(4,1)S(1)}, s32[]{:S(2)}) async-start(s8[4718592]{0:T(1024)(128)(4,1)} %bitcast.45), calls=%async_computation.8 | async-start | bytes 1048576
  106.4 65.0 %reduce-scatter.8.cloned.1.call-start = ((), (), s32[]{:S(2)}) async-start(), calls=%async_computation.3 | async-start | bytes 5898240 | tf_op jit(solution)/shard_map/reduce_scatter | solution.py:71
  127.5 9.3 %collective-permute-start.1 = (bf16[128,1152]{1,0:T(8,128)(2,1)S(1)}, bf16[128,1152]{1,0:T(8,128)(2,1)S(1)}, u32[]{:S(2)}, u32[]{:S(2)}) collective-permute-start(bf16[128,1152]{1,0:T(8,128)(2,1)S(1)} %add_convert_fusion), channel_id=1, source_target_pairs={{8,0},{16,8},{24,16},{9,1},{17,9},{25,17},{10,2},{18,10},{26,18},{... | collective-permute-start | bytes 884744 | tf_op jit(solution)/shard_map/ppermute | solution.py:12
Sparse Core Ops, SparseCore 0:
  9.5 40.1 all-gather.2
  57.7 15.3 reduce-scatter.9
  106.5 14.4 reduce-scatter.11
  123.4 47.9 reduce-scatter.7
where the time goes:
time: 182 us
  waiting for transfers between devices  99.5 us (55%)
  blocking collectives  24.8 us (14%)
  between operations  17.8 us (10%)
  matrix products  17.5 us (10%)
  other arithmetic  12.6 us (7%)
  local copies, waits for them, and re-layouts  6.68 us (4%)
  starting transfers between devices  2.88 us (2%)
    all_gather x1, waiting for transfers between devices, per_device(): full_weight = lax.all_gather(weight[0], 'fsdp', axis=0, tiled=True)  32 us
    reduce_scatter x1, waiting for transfers between devices, per_device(): lax.psum_scatter(lax.dot_general(lhs_all, rhs_all, (((0,), (0,)), ((), ()...  27.2 us
    unnamed x6, waiting for transfers between devices  24.3 us
    ppermute x2, waiting for transfers between devices, shifted(): return lax.ppermute(shard, axis, pairs)  16 us
    all_gather x2, blocking collectives, per_device(): grad_in = lax.all_gather(held_share, 'tp', axis=1, tiled=True)  14.9 us
    psum x2, blocking collectives, per_device(): moment_sum = lax.psum(jnp.sum(gained * scaled_share, axis=-1), 'tp')  9.85 us
    dot_general x2, matrix products, per_device(): products = jnp.dot(stacked, full_weight, preferred_element_type=jnp.float32)  7.83 us
    dot_general x1, matrix products, per_device(): lax.dot_general(lhs_all, rhs_all, (((0,), (0,)), ((), ())), preferred_ele...  6.34 us
  transfers between devices with their start and end apart: 6, of which 6 were waited for; matrix products, arithmetic and copies ran while one was open for 8% of the time, Pallas kernels for 0%

commit v1 on v0

--- a/solution.py
+++ b/solution.py
@@ -57,7 +57,9 @@
         gain_share = lax.dynamic_slice_in_dim(section_gain, share_start, share_width, 0)
         grad_share = lax.dynamic_slice_in_dim(grad_in, share_start, share_width, 1)
         gained = gain_share * total_share
-        moment_sum = lax.psum(jnp.sum(gained * scaled_share, axis=-1), "tp")
+        moment_sum = jnp.sum(
+            lax.all_gather(jnp.sum(gained * scaled_share, axis=-1), axis_name="tp"), axis=0
+        )
         inner_mean = (moment_sum / feature_count)[:, None]
         out_share = (
             grad_share.astype(jnp.float32) + inv_rms * (gained - scaled_share * inner_mean)

time: 182 us -> 182 us (level)
    psum x2 -> x0, blocking collectives: 9.85 us -> none  [per_device(): moment_sum = lax.psum(jnp.sum(gained * scaled_share, axis=-1), 'tp')]
    all_gather x0 -> x2, blocking collectives: none -> 8.46 us  [per_device(): lax.all_gather(jnp.sum(gained * scaled_share, axis=-1), axis_name='tp')]
where the time goes in v1:
time: 182 us; the launch traced here: 181 us
  waiting for transfers between devices  100 us (55%)
  blocking collectives  23.4 us (13%)
  between operations  17.8 us (10%)
  matrix products  17.5 us (10%)
  other arithmetic  12.6 us (7%)
  local copies, waits for them, and re-layouts  6.68 us (4%)
  starting transfers between devices  2.88 us (2%)
    all_gather x1, waiting for transfers between devices, per_device(): full_weight = lax.all_gather(weight[0], 'fsdp', axis=0, tiled=True)  32 us
    reduce_scatter x1, waiting for transfers between devices, per_device(): lax.psum_scatter(lax.dot_general(lhs_all, rhs_all, (((0,), (0,)), ((), ()...  27.8 us
    unnamed x6, waiting for transfers between devices  24.3 us
    ppermute x2, waiting for transfers between devices, shifted(): return lax.ppermute(shard, axis, pairs)  16 us
    all_gather x2, blocking collectives, per_device(): grad_in = lax.all_gather(held_share, 'tp', axis=1, tiled=True)  14.9 us
    all_gather x2, blocking collectives, per_device(): lax.all_gather(jnp.sum(gained * scaled_share, axis=-1), axis_name='tp')  8.46 us
    dot_general x2, matrix products, per_device(): products = jnp.dot(stacked, full_weight, preferred_element_type=jnp.float32)  7.83 us
    dot_general x1, matrix products, per_device(): lax.dot_general(lhs_all, rhs_all, (((0,), (0,)), ((), ())), preferred_ele...  6.34 us
  transfers between devices with their start and end apart: 6, of which 6 were waited for; matrix products, arithmetic and copies ran while one was open for 8% of the time, Pallas kernels for 0%

profile of v1, /device:TPU:0, one launch (start us, length us, event | category | flops | bytes accessed | tf_op | source)
XLA Modules:
  0.0 181.0 jit_solution(15712405206883271262)
XLA Ops:
  7.2 0.0 all-gather.7.cloned.1.call-start
  7.2 0.7 all-gather.7.cloned.1.call-update
  7.9 0.0 reduce-scatter.10.cloned.1.call-start
  7.9 1.3 fusion.55
  11.8 0.7 reduce.3
  13.9 1.6 fusion.22
  15.5 2.3 %multiply_convert_fusion = (bf16[128,2304]{1,0:T(8,128)(2,1)}, bf16[128,2304]{1,0:T(8,128)(2,1)S(1)}, f32[128,2304]{1,0:T(8,128)S(1)}, f32[128,2304]{1,0:T(8,128)S(1)}) fusion(f32[2304]{0:T(1024)S(1)} %reduce.3, f32[128]{0:T(128)S(1)} %get-tuple-element.16, bf16[1,4,128,2304]{3,2,1,0:T(8,128)(2,1)} %param.6, s32[]{:T(128)S(6)} %select_n.33, ...), kind=kLoop, calls=%fused_computation.31 | loop fusion | flops 2359296 | bytes 4728840 | tf_op jit(solution)/shard_map/convert_element_type | solution.py:38
  17.7 32.0 %all-gather.7.cloned.1.call-done = bf16[1,2304,1024]{2,1,0:T(8,128)(2,1)} async-done(((bf16[1,576,1024]{2,1,0:T(8,128)(2,1)}), bf16[1,2304,1024]{2,1,0:T(8,128)(2,1)}) %all-gather.7.cloned.1.call-update) | async-done | bytes 4718608 | tf_op jit(solution)/shard_map/all_gather | solution.py:20
  49.7 4.0 %fusion.6 = f32[256,1024]{1,0:T(8,128)S(1)} fusion(bf16[1,2304,1024]{2,1,0:T(8,128)(2,1)} %all-gather.7.cloned.1.call-done, bf16[128,2304]{1,0:T(8,128)(2,1)} %bitcast.54, bf16[128,2304]{1,0:T(8,128)(2,1)S(1)} %get-tuple-element.5), kind=kOutput, calls=%fused_computation.7 | convolution fusion | flops 1210318848 | bytes 6946816 | tf_op jit(solution)/shard_map/dot_general | solution.py:40
  53.8 0.0 copy-done.3
  53.8 1.1 multiply_convert_fusion.3
  54.9 0.0 copy-done
  54.9 1.7 fusion.8
  56.5 1.1 copy.8
  57.6 0.0 reduce-scatter.10.cloned.1.call-update
  57.6 0.0 reduce-scatter.12.cloned.1.call-start
  57.7 15.4 %reduce-scatter.10.cloned.1.call-done = bf16[1152,128]{1,0:T(8,128)(2,1)} async-done(((bf16[2304,128]{1,0:T(8,128)(2,1)}), bf16[1152,128]{1,0:T(8,128)(2,1)}) %reduce-scatter.10.cloned.1.call-update) | async-done | bytes 294928
  73.1 1.2 copy.9
  74.3 0.2 multiply_reduce_fusion.1
  74.5 4.2 %all-gather.3 = f32[2,1,128]{2,1,0:T(1,128)S(1)} all-gather(f32[1,1,128]{2,1,0:T(1,128)S(1)} %bitcast.56), channel_id=3, replica_groups=mesh['section'=4,'fsdp'=4,'tp'=2] {'tp'}, dimensions={0}, use_global_device_ids=true | all-gather | bytes 1536 | tf_op jit(solution)/shard_map/all_gather | solution.py:61
  78.7 1.3 fusion.36
  80.0 0.0 copy-start.2
  80.0 1.4 collective-permute-start
  81.4 0.1 fusion.54
  81.5 8.0 %collective-permute-done = bf16[128,1152]{1,0:T(8,128)(2,1)} collective-permute-done((bf16[128,1152]{1,0:T(8,128)(2,1)S(1)}, bf16[128,1152]{1,0:T(8,128)(2,1)}, u32[]{:S(2)}, u32[]{:S(2)}) %collective-permute-start) | collective-permute-done | bytes 294944 | tf_op jit(solution)/shard_map/ppermute | solution.py:12
  89.5 1.0 bitcast_select_fusion
  90.6 0.0 slice-start
  90.6 7.5 %all_gather.24 = bf16[128,2304]{1,0:T(8,128)(2,1)S(1)} all-gather(bf16[128,1152]{1,0:T(8,128)(2,1)S(1)} %bitcast_select_fusion), channel_id=1, replica_groups=mesh['section'=4,'fsdp'=4,'tp'=2] {'tp'}, dimensions={1}, use_global_device_ids=true | all-gather | bytes 884736 | tf_op jit(solution)/shard_map/all_gather | solution.py:70
  98.1 3.8 %fusion.2 = f32[256,1024]{1,0:T(8,128)S(1)} fusion(bf16[1,2304,1024]{2,1,0:T(8,128)(2,1)} %all-gather.7.cloned.1.call-done, bf16[128,2304]{1,0:T(8,128)(2,1)S(1)} %all_gather.24, bf16[128,2304]{1,0:T(8,128)(2,1)S(1)} %copy-done.2), kind=kOutput, calls=%fused_computation.3 | convolution fusion | flops 1210318848 | bytes 6946816 | tf_op jit(solution)/shard_map/dot_general | solution.py:40
  101.9 1.1 multiply_convert_fusion.2
  103.0 1.7 fusion.11
  104.7 1.1 copy.10
  105.7 0.0 reduce-scatter.12.cloned.1.call-update
  105.7 0.0 reduce-scatter.8.cloned.1.call-start
  105.8 6.3 %convolution_convert_fusion = bf16[2304,1024]{1,0:T(8,128)(2,1)} fusion(bf16[128,2304]{1,0:T(8,128)(2,1)S(1)} %all_gather.24, bf16[128,2304]{1,0:T(8,128)(2,1)} %get-tuple-element.4, bf16[128,2304]{1,0:T(8,128)(2,1)} %bitcast.55, bf16[128,2304]{1,0:T(8,128)(2,1)} %copy-done.3, bf16[128,1024]{1,0:T(8,128)(2,1)} %get-tuple-element.12, ...), kind=kOutput, calls=%fused_computation | convolution fusion | flops 2431909888 | bytes 8126464 | tf_op jit(solution)/shard_map/dot_general | solution.py:74
  112.1 0.0 reduce-scatter.8.cloned.1.call-update
  112.2 8.2 %reduce-scatter.12.cloned.1.call-done = bf16[1152,128]{1,0:T(8,128)(2,1)} async-done(((bf16[2304,128]{1,0:T(8,128)(2,1)}), bf16[1152,128]{1,0:T(8,128)(2,1)}) %reduce-scatter.12.cloned.1.call-update) | async-done | bytes 294928
  120.4 1.2 copy.11
  121.5 0.2 multiply_reduce_fusion
  121.7 4.2 %all-gather.4 = f32[2,1,128]{2,1,0:T(1,128)S(1)} all-gather(f32[1,1,128]{2,1,0:T(1,128)S(1)} %bitcast.57), channel_id=4, replica_groups=mesh['section'=4,'fsdp'=4,'tp'=2] {'tp'}, dimensions={0}, use_global_device_ids=true | all-gather | bytes 1536 | tf_op jit(solution)/shard_map/all_gather | solution.py:61
  125.9 0.2 add_convert_fusion
  126.1 1.3 collective-permute-start.1
  127.4 8.0 %collective-permute-done.1 = bf16[128,1152]{1,0:T(8,128)(2,1)S(1)} collective-permute-done((bf16[128,1152]{1,0:T(8,128)(2,1)S(1)}, bf16[128,1152]{1,0:T(8,128)(2,1)S(1)}, u32[]{:S(2)}, u32[]{:S(2)}) %collective-permute-start.1) | collective-permute-done | bytes 294944 | tf_op jit(solution)/shard_map/ppermute | solution.py:12
  135.5 0.1 bitcast_select_fusion.1
  135.5 7.4 %all_gather.27 = bf16[128,2304]{1,0:T(8,128)(2,1)S(1)} all-gather(bf16[128,1152]{1,0:T(8,128)(2,1)S(1)} %bitcast_select_fusion.1), channel_id=1, replica_groups=mesh['section'=4,'fsdp'=4,'tp'=2] {'tp'}, dimensions={1}, use_global_device_ids=true | all-gather | bytes 884736 | tf_op jit(solution)/shard_map/all_gather | solution.py:70
  142.9 27.8 %reduce-scatter.8.cloned.1.call-done = bf16[576,1024]{1,0:T(8,128)(2,1)} async-done(((bf16[2304,1024]{1,0:T(8,128)(2,1)}), bf16[576,1024]{1,0:T(8,128)(2,1)}) %reduce-scatter.8.cloned.1.call-update) | async-done | bytes 1179664 | tf_op jit(solution)/shard_map/reduce_scatter | solution.py:73
  170.7 3.0 %bitcast_convert_fusion = f32[1,576,1024]{2,1,0:T(8,128)} fusion(bf16[576,1024]{1,0:T(8,128)(2,1)} %reduce-scatter.8.cloned.1.call-done), kind=kLoop, calls=%fused_computation.30 | loop fusion | flops 589824 | bytes 3538944 | tf_op jit(solution)/shard_map/broadcast_in_dim | solution.py:81
  173.7 0.8 copy.13
  (17 shorter events, 0.1 us)
Async XLA Ops:
  7.2 42.6 %all-gather.7.cloned.1.call-start = ((), (), s32[]{:S(2)}) async-start(), calls=%async_computation.4 | async-start | bytes 5898240 | tf_op jit(solution)/shard_map/all_gather | solution.py:20
  7.9 65.2 %reduce-scatter.10.cloned.1.call-start = ((), (), s32[]{:S(2)}) async-start(), calls=%async_computation.5 | async-start | bytes 884736
  17.7 36.1 %copy-start.3 = (bf16[128,2304]{1,0:T(8,128)(2,1)}, bf16[128,2304]{1,0:T(8,128)(2,1)S(1)}, u32[]{:S(2)}) copy-start(bf16[128,2304]{1,0:T(8,128)(2,1)S(1)} %get-tuple-element.5) | copy-start | bytes 1769476
  49.7 5.1 %copy-start = (bf16[1,2304,1024]{2,1,0:T(8,128)(2,1)S(1)}, bf16[1,2304,1024]{2,1,0:T(8,128)(2,1)}, u32[]{:S(2)}) copy-start(bf16[1,2304,1024]{2,1,0:T(8,128)(2,1)} %all-gather.7.cloned.1.call-done) | copy-start | bytes 14155780
  54.9 2.8 %copy-start.4 = (f32[1,2304]{1,0:T(1,128)S(1)}, f32[1,2304]{1,0:T(1,128)}, u32[]{:S(2)}) copy-start(f32[1,2304]{1,0:T(1,128)} %param.10) | copy-start | bytes 27652
  57.6 62.7 %reduce-scatter.12.cloned.1.call-start = ((), (), s32[]{:S(2)}) async-start(), calls=%async_computation.6 | async-start | bytes 884736
  78.7 2.7 %copy-start.1 = (bf16[2,128,2304]{2,1,0:T(8,128)(2,1)S(1)}, bf16[2,128,2304]{2,1,0:T(8,128)(2,1)}, u32[]{:S(2)}) copy-start(bf16[2,128,2304]{2,1,0:T(8,128)(2,1)} %param.8) | copy-start | bytes 3538948
  80.0 18.1 %copy-start.2 = (bf16[128,2304]{1,0:T(8,128)(2,1)S(1)}, bf16[128,2304]{1,0:T(8,128)(2,1)}, u32[]{:S(2)}) copy-start(bf16[128,2304]{1,0:T(8,128)(2,1)} %get-tuple-element.4) | copy-start | bytes 1769476
  80.0 9.5 %collective-permute-start = (bf16[128,1152]{1,0:T(8,128)(2,1)S(1)}, bf16[128,1152]{1,0:T(8,128)(2,1)}, u32[]{:S(2)}, u32[]{:S(2)}) collective-permute-start(bf16[128,1152]{1,0:T(8,128)(2,1)S(1)} %fusion.36), channel_id=1, source_target_pairs={{8,0},{16,8},{24,16},{9,1},{17,9},{25,17},{10,2},{18,10},{26,18},{... | collective-permute-start | bytes 884744 | tf_op jit(solution)/shard_map/ppermute | solution.py:12
  90.6 12.4 %slice-start = ((s8[4718592]{0:T(1024)(128)(4,1)}), s8[4194304]{0:T(1024)(128)(4,1)S(1)}, s32[]{:S(2)}) async-start(s8[4718592]{0:T(1024)(128)(4,1)} %bitcast.47), calls=%async_computation.7 | async-start | bytes 8388608
  98.1 4.9 %slice-start.1 = ((s8[4718592]{0:T(1024)(128)(4,1)}), s8[524288]{0:T(1024)(128)(4,1)S(1)}, s32[]{:S(2)}) async-start(s8[4718592]{0:T(1024)(128)(4,1)} %bitcast.47), calls=%async_computation.8 | async-start | bytes 1048576
  105.7 65.0 %reduce-scatter.8.cloned.1.call-start = ((), (), s32[]{:S(2)}) async-start(), calls=%async_computation.3 | async-start | bytes 5898240 | tf_op jit(solution)/shard_map/reduce_scatter | solution.py:73
  126.1 9.3 %collective-permute-start.1 = (bf16[128,1152]{1,0:T(8,128)(2,1)S(1)}, bf16[128,1152]{1,0:T(8,128)(2,1)S(1)}, u32[]{:S(2)}, u32[]{:S(2)}) collective-permute-start(bf16[128,1152]{1,0:T(8,128)(2,1)S(1)} %add_convert_fusion), channel_id=1, source_target_pairs={{8,0},{16,8},{24,16},{9,1},{17,9},{25,17},{10,2},{18,10},{26,18},{... | collective-permute-start | bytes 884744 | tf_op jit(solution)/shard_map/ppermute | solution.py:12
Sparse Core Ops, SparseCore 0:
  9.5 40.1 all-gather.6
  57.7 15.3 reduce-scatter.9
  105.9 14.4 reduce-scatter.11
  122.7 47.9 reduce-scatter.7
